TPU v7x, 32 devices: a whole 2x2x4 slice. The times are simulated.
32 devices in a mesh: xy: 2 (over core), gz: 4 (over y, x), ta: 4 (over z).
Axes of the slice: x: 2, y: 2, z: 4, core: 2. Of those that a mesh axis runs over, the one named last changes fastest.
Arguments:
- right_side: float32 [2, 4, 4, 128, 128], P('xy', 'gz', 'ta'), may hold values from -40 to 40
- link_blocks: float32 [2, 4, 4, 9, 2, 32, 32, 128], P('xy', 'gz', 'ta'), may hold values from -0.75 to 0.75
Outputs:
- solution: float32 [2, 4, 4, 128, 128], P('xy', 'gz', 'ta')
- residual: float32 [2, 4, 4, 128, 128], P('xy', 'gz', 'ta')
All inputs are finite; a program needn't handle non-finite values.
Results may differ from a plain program's by a relative error of at most 0.00018.
Values sent between devices are 32-bit elements; how exact they have to be, the bound alone decides.
A program may use at most 128 MiB of HBM per device.

v0:
```python
import jax
import jax.numpy as jnp
from jax import lax
from jax.sharding import PartitionSpec as P

DOF = 32
RHS = 2
CX = 1
NY = 8
CZ = 2
CT = 8
ITERS = 2


mass_shift = 4.0
epsilon = 1e-06


def padded_2(cells, sides, width):
    for axis, dim in sides:
        count = lax.axis_size(axis)
        head = lax.slice_in_dim(cells, 0, width, axis=dim)
        tail = lax.slice_in_dim(cells, cells.shape[dim] - width, cells.shape[dim], axis=dim)
        cells = jnp.concatenate(
            [
                lax.ppermute(tail, axis, [(i, (i + 1) % count) for i in range(count)]),
                cells,
                lax.ppermute(head, axis, [((i + 1) % count, i) for i in range(count)]),
            ],
            axis=dim,
        )
    return cells


def split_parts(joined):
    shaped = joined.reshape(joined.shape[:-1] + (RHS, 2, DOF))
    return (shaped[..., 0, :], shaped[..., 1, :])


def join_parts(real, imaginary):
    stacked = jnp.stack((real, imaginary), -2)
    return stacked.reshape(stacked.shape[:-3] + (-1,))


def column_sums(values):
    folded = jnp.sum(values, axis=-1)
    return jnp.sum(folded.reshape(-1, folded.shape[-1]), axis=0)


def stacked_product(blocks, field):
    return jnp.einsum("...kcds,...ksrd->...src", blocks, field, precision=lax.Precision.HIGHEST)


def apply_operator(link_blocks, real, imaginary):
    joined = join_parts(real, imaginary)
    grid = joined.reshape(CX, NY, CZ, CT, joined.shape[-1])
    padded = padded_2(grid, (("xy", 0), ("gz", 2), ("ta", 3)), 1)
    nearby = [
        grid,
        padded[2:, :, 1:-1, 1:-1],
        padded[:-2, :, 1:-1, 1:-1],
        jnp.roll(grid, -1, 1),
        jnp.roll(grid, 1, 1),
        padded[1:-1, :, 2:, 1:-1],
        padded[1:-1, :, :-2, 1:-1],
        padded[1:-1, :, 1:-1, 2:],
        padded[1:-1, :, 1:-1, :-2],
    ]
    stacked = jnp.stack([piece.reshape(joined.shape) for piece in nearby], -3)
    near_real, near_imag = split_parts(stacked)
    blocks_real = link_blocks[..., 0, :, :, :]
    blocks_imag = link_blocks[..., 1, :, :, :]
    out_real = (
        mass_shift * real
        + stacked_product(blocks_real, near_real)
        - stacked_product(blocks_imag, near_imag)
    )
    output_imaginary = (
        mass_shift * imaginary
        + stacked_product(blocks_real, near_imag)
        + stacked_product(blocks_imag, near_real)
    )
    return (out_real, output_imaginary)


def project_out(basis, work_real, work_imag, proj_real, proj_imag):
    for index in range(len(basis)):
        coef_real = proj_real[index][:, None]
        coef_imag = proj_imag[index][:, None]
        vector = basis[index]
        work_real = work_real - (coef_real * vector[0] - coef_imag * vector[1])
        work_imag = work_imag - (coef_real * vector[1] + coef_imag * vector[0])
    return (work_real, work_imag)


def solve_positive_definite(matrix, target):
    size = matrix.shape[0]
    lower = {}
    for row in range(size):
        for col in range(row + 1):
            value = matrix[row, col]
            for inner in range(col):
                value = value - lower[row, inner] * lower[col, inner]
            if row == col:
                lower[row, row] = jnp.sqrt(value)
            else:
                lower[row, col] = value / lower[col, col]
    forward = []
    for row in range(size):
        value = target[row]
        for inner in range(row):
            value = value - lower[row, inner] * forward[inner]
        forward.append(value / lower[row, row])
    answer = [None] * size
    for row in reversed(range(size)):
        value = forward[row]
        for inner in range(row + 1, size):
            value = value - lower[inner, row] * answer[inner]
        answer[row] = value / lower[row, row]
    return jnp.stack(answer)


def least_squares(hessenberg_real, hessenberg_imaginary, beta):
    exact_answer_vector = lax.Precision.HIGHEST
    gram_matrix_real = jnp.einsum(
        "sxm,szm->xzm", hessenberg_real, hessenberg_real, precision=exact_answer_vector
    ) + jnp.einsum(
        "sxm,szm->xzm", hessenberg_imaginary, hessenberg_imaginary, precision=exact_answer_vector
    )
    gram_matrix_imaginary = jnp.einsum(
        "sxm,szm->xzm", hessenberg_real, hessenberg_imaginary, precision=exact_answer_vector
    ) - jnp.einsum(
        "sxm,szm->xzm", hessenberg_imaginary, hessenberg_real, precision=exact_answer_vector
    )
    upper = jnp.concatenate((gram_matrix_real, -gram_matrix_imaginary), 1)
    bottom = jnp.concatenate((gram_matrix_imaginary, gram_matrix_real), 1)
    system = jnp.concatenate((upper, bottom), 0)
    target = jnp.concatenate(
        (beta[None, :] * hessenberg_real[0], -beta[None, :] * hessenberg_imaginary[0]), 0
    )
    answer = solve_positive_definite(system, target)
    return (answer[:ITERS], answer[ITERS:])


def shards(right_side, link_blocks):
    rhs_real, rhs_imag = split_parts(right_side)
    start_sum = lax.psum(column_sums(rhs_real * rhs_real + rhs_imag * rhs_imag), ("xy", "gz", "ta"))
    beta = jnp.sqrt(start_sum + epsilon)
    basis = [(rhs_real / beta[:, None], rhs_imag / beta[:, None])]
    hessenberg_real = jnp.zeros((ITERS + 1, ITERS, RHS), jnp.float32)
    hessenberg_imaginary = jnp.zeros((ITERS + 1, ITERS, RHS), jnp.float32)
    for step in range(ITERS):
        work_real, work_imag = apply_operator(link_blocks, basis[step][0], basis[step][1])
        proj_real = jnp.stack(
            [column_sums(vector[0] * work_real + vector[1] * work_imag) for vector in basis]
        )
        proj_imag = jnp.stack(
            [column_sums(vector[0] * work_imag - vector[1] * work_real) for vector in basis]
        )
        proj_real, proj_imag = lax.psum((proj_real, proj_imag), ("xy", "gz", "ta"))
        work_real, work_imag = project_out(basis, work_real, work_imag, proj_real, proj_imag)
        leftover = lax.psum(
            column_sums(work_real * work_real + work_imag * work_imag), ("xy", "gz", "ta")
        )
        norm = jnp.sqrt(leftover + epsilon)
        hessenberg_real = hessenberg_real.at[: step + 1, step].set(proj_real)
        hessenberg_imaginary = hessenberg_imaginary.at[: step + 1, step].set(proj_imag)
        hessenberg_real = hessenberg_real.at[step + 1, step].set(norm)
        basis.append((work_real / norm[:, None], work_imag / norm[:, None]))
    coef_real, coef_imag = least_squares(hessenberg_real, hessenberg_imaginary, beta)
    sol_real = jnp.zeros_like(rhs_real)
    sol_imag = jnp.zeros_like(rhs_imag)
    for index in range(ITERS):
        weight_real = coef_real[index][:, None]
        weight_imag = coef_imag[index][:, None]
        sol_real = sol_real + weight_real * basis[index][0] - weight_imag * basis[index][1]
        sol_imag = sol_imag + weight_real * basis[index][1] + weight_imag * basis[index][0]
    exact_answer_vector = lax.Precision.HIGHEST
    mixed_real = jnp.einsum(
        "ijr,jr->ir", hessenberg_real, coef_real, precision=exact_answer_vector
    ) - jnp.einsum("ijr,jr->ir", hessenberg_imaginary, coef_imag, precision=exact_answer_vector)
    mixed_imag = jnp.einsum(
        "ijr,jr->ir", hessenberg_real, coef_imag, precision=exact_answer_vector
    ) + jnp.einsum("ijr,jr->ir", hessenberg_imaginary, coef_real, precision=exact_answer_vector)
    image_real = jnp.zeros_like(rhs_real)
    image_imag = jnp.zeros_like(rhs_imag)
    for index in range(ITERS + 1):
        weight_real = mixed_real[index][:, None]
        weight_imag = mixed_imag[index][:, None]
        image_real = image_real + weight_real * basis[index][0] - weight_imag * basis[index][1]
        image_imag = image_imag + weight_real * basis[index][1] + weight_imag * basis[index][0]
    return (
        join_parts(sol_real, sol_imag),
        join_parts(rhs_real - image_real, rhs_imag - image_imag),
    )


def solution(mesh):
    return jax.shard_map(
        shards,
        mesh=mesh,
        in_specs=(
            P("xy", "gz", "ta", None, None),
            P("xy", "gz", "ta", None, None, None, None, None),
        ),
        out_specs=(P("xy", "gz", "ta", None, None), P("xy", "gz", "ta", None, None)),
        check_vma=False,
    )
```

profile of v0, /device:TPU:0, one launch (start us, length us, event | category | flops | bytes accessed | tf_op | source)
XLA Modules:
  0.0 448.2 jit_solution(8426197218118782616)
XLA Ops:
  1.7 41.9 %psum.49 = f32[2]{0:T(128)S(1)} all-reduce(f32[2]{0:T(128)S(1)} %fusion.45), channel_id=1, replica_groups=mesh['xy'=2,'gz'=4,'ta'=4] {'xy','gz','ta'}, use_global_device_ids=true, to_apply=%region_1.0 | all-reduce | flops 2 | bytes 16 | tf_op jit(solution)/shard_map/psum | solution.py:147
  45.5 8.9 %fusion.66 = (f32[1,1,1,9,1,32,32,128]{7,6,5,4,3,2,1,0:T(8,128)}, f32[1,1,1,9,1,32,32,128]{7,6,5,4,3,2,1,0:T(8,128)}) fusion(f32[1,1,1,9,2,32,32,128]{7,6,5,4,3,2,1,0:T(8,128)} %param.15), kind=kLoop, calls=%fused_computation.209 | loop fusion | bytes 18874368 | tf_op jit(solution)/shard_map/slice | solution.py:71
  54.3 15.9 %copy.256 = f32[1,1,1,9,1,32,32,128]{6,5,3,7,4,2,1,0:T(8,128)} copy(f32[1,1,1,9,1,32,32,128]{7,6,5,4,3,2,1,0:T(8,128)} %get-tuple-element.132) | data formatting | bytes 9437184
  70.3 16.0 %copy.257 = f32[1,1,1,9,1,32,32,128]{6,5,3,7,4,2,1,0:T(8,128)} copy(f32[1,1,1,9,1,32,32,128]{7,6,5,4,3,2,1,0:T(8,128)} %get-tuple-element.133) | data formatting | bytes 9437184
  86.9 2.3 collective-permute-start.2
  90.1 2.3 collective-permute-done.2
  92.4 3.1 collective-permute-done.3
  95.6 2.3 collective-permute-start.4
  97.9 1.9 collective-permute-done.4
  99.7 4.0 collective-permute-done.5
  105.4 1.4 copy.168
  107.9 20.3 %fusion.16 = f32[128,2,32]{2,1,0:T(2,128)S(1)} fusion(f32[9,128,2,32]{3,2,0,1:T(2,128)S(1)} %copy.168, f32[1,1,1,9,1,32,32,128]{6,5,3,7,4,2,1,0:T(8,128)} %copy.256), kind=kOutput, calls=%fused_computation.16 | convolution fusion | flops 28311552 | bytes 5046272 | tf_op jit(solution)/shard_map/...kcds,...ksrd->...src/dot_general | solution.py:51
  128.3 17.2 %fusion.19 = f32[128,2,32]{2,1,0:T(2,128)S(1)} fusion(f32[9,128,2,32]{3,2,0,1:T(2,128)S(1)} %copy.171, f32[1,1,1,9,1,32,32,128]{6,5,3,7,4,2,1,0:T(8,128)S(1)} %copy-done), kind=kOutput, calls=%fused_computation.17 | convolution fusion | flops 28311552 | bytes 5046272 | tf_op jit(solution)/shard_map/...kcds,...ksrd->...src/dot_general | solution.py:51
  145.5 19.6 %fusion.28 = f32[128,2,32]{2,1,0:T(2,128)S(1)} fusion(f32[9,128,2,32]{3,2,0,1:T(2,128)S(1)} %copy.171, f32[1,1,1,9,1,32,32,128]{6,5,3,7,4,2,1,0:T(8,128)} %copy.257), kind=kOutput, calls=%fused_computation.20 | convolution fusion | flops 28311552 | bytes 5046272 | tf_op jit(solution)/shard_map/...kcds,...ksrd->...src/dot_general | solution.py:51
  165.1 17.4 %fusion.31 = f32[128,2,32]{2,1,0:T(2,128)S(1)} fusion(f32[9,128,2,32]{3,2,0,1:T(2,128)S(1)} %copy.168, f32[1,1,1,9,1,32,32,128]{6,5,3,7,4,2,1,0:T(8,128)S(1)} %bitcast.515), kind=kOutput, calls=%fused_computation.21 | convolution fusion | flops 28311552 | bytes 5046272 | tf_op jit(solution)/shard_map/...kcds,...ksrd->...src/dot_general | solution.py:51
  183.0 36.8 %all-reduce.3 = (f32[1,2]{1,0:T(1,128)S(1)}, f32[1,2]{1,0:T(1,128)S(1)}) all-reduce(f32[1,2]{1,0:T(1,128)S(1)} %bitcast.540, f32[1,2]{1,0:T(1,128)S(1)} %bitcast.539), channel_id=1, replica_groups=mesh['xy'=2,'gz'=4,'ta'=4] {'xy','gz','ta'}, use_global_device_ids=true, to_apply=%region_5.6 | all-reduce | flops 4 | bytes 32 | tf_op jit(solution)/shard_map/psum | solution.py:160
  220.0 41.4 %psum.52 = f32[2]{0:T(128)S(1)} all-reduce(f32[2]{0:T(128)S(1)} %get-tuple-element.129), channel_id=1, replica_groups=mesh['xy'=2,'gz'=4,'ta'=4] {'xy','gz','ta'}, use_global_device_ids=true, to_apply=%region_7.8 | all-reduce | flops 2 | bytes 16 | tf_op jit(solution)/shard_map/psum | solution.py:162
  263.4 3.1 collective-permute-start.8
  267.4 2.4 collective-permute-done.8
  269.8 2.6 collective-permute-done.9
  272.4 1.6 collective-permute-start.10
  274.5 2.1 collective-permute-done.10
  276.6 3.3 collective-permute-done.11
  281.5 1.6 copy.218
  283.1 19.4 %fusion.37 = f32[128,2,32]{2,1,0:T(2,128)S(1)} fusion(f32[9,128,2,32]{3,2,0,1:T(2,128)S(1)} %copy.218, f32[1,1,1,9,1,32,32,128]{6,5,3,7,4,2,1,0:T(8,128)} %copy.257), kind=kOutput, calls=%fused_computation.23 | convolution fusion | flops 28311552 | bytes 5046272 | tf_op jit(solution)/shard_map/...kcds,...ksrd->...src/dot_general | solution.py:51
  302.5 19.4 %fusion.22 = f32[128,2,32]{2,1,0:T(2,128)S(1)} fusion(f32[9,128,2,32]{3,2,0,1:T(2,128)S(1)} %copy.218, f32[1,1,1,9,1,32,32,128]{6,5,3,7,4,2,1,0:T(8,128)} %copy.256), kind=kOutput, calls=%fused_computation.18 | convolution fusion | flops 28311552 | bytes 5046272 | tf_op jit(solution)/shard_map/...kcds,...ksrd->...src/dot_general | solution.py:51
  323.1 19.4 %fusion.25 = f32[128,2,32]{2,1,0:T(2,128)S(1)} fusion(f32[9,128,2,32]{3,2,0,1:T(2,128)S(1)} %copy.221, f32[1,1,1,9,1,32,32,128]{6,5,3,7,4,2,1,0:T(8,128)} %copy.256), kind=kOutput, calls=%fused_computation.19 | convolution fusion | flops 28311552 | bytes 5046272 | tf_op jit(solution)/shard_map/...kcds,...ksrd->...src/dot_general | solution.py:51
  342.5 19.6 %fusion.34 = f32[128,2,32]{2,1,0:T(2,128)S(1)} fusion(f32[9,128,2,32]{3,2,0,1:T(2,128)S(1)} %copy.221, f32[1,1,1,9,1,32,32,128]{6,5,3,7,4,2,1,0:T(8,128)} %copy.257), kind=kOutput, calls=%fused_computation.22 | convolution fusion | flops 28311552 | bytes 5046272 | tf_op jit(solution)/shard_map/...kcds,...ksrd->...src/dot_general | solution.py:51
  362.7 36.9 %all-reduce.2 = (f32[2,2]{1,0:T(2,128)S(1)}, f32[2,2]{1,0:T(2,128)S(1)}) all-reduce(f32[2,2]{1,0:T(2,128)S(1)} %pad_maximum_fusion.31, f32[2,2]{1,0:T(2,128)S(1)} %pad_maximum_fusion.30), channel_id=1, replica_groups=mesh['xy'=2,'gz'=4,'ta'=4] {'xy','gz','ta'}, use_global_device_ids=true, to_apply=%region_13.14 | all-reduce | flops 8 | bytes 64 | tf_op jit(solution)/shard_map/psum | solution.py:160
  399.8 42.2 %psum.55 = f32[2]{0:T(128)S(1)} all-reduce(f32[2]{0:T(128)S(1)} %add_reduce_fusion), channel_id=1, replica_groups=mesh['xy'=2,'gz'=4,'ta'=4] {'xy','gz','ta'}, use_global_device_ids=true, to_apply=%region_15.16 | all-reduce | flops 2 | bytes 16 | tf_op jit(solution)/shard_map/psum | solution.py:162
  442.0 1.3 scatter.24
  443.4 1.3 scatter.29
  (162 shorter events, 17.8 us)
Async XLA Ops:
  44.1 42.7 %collective-permute-start.1 = (f32[1,8,2,8,128]{4,3,2,1,0:T(8,128)S(1)}, f32[1,8,2,8,128]{4,3,2,1,0:T(8,128)S(1)}, u32[]{:S(2)}, u32[]{:S(2)}) collective-permute-start(f32[1,8,2,8,128]{4,3,2,1,0:T(8,128)S(1)} %reshape_reshape.6), channel_id=1, source_target_pairs={{0,16},{16,0},{1,17},{17,1},{2,18},{18,2},{3,19},{19,3},{4,20},{20... | collective-permute-start | bytes 196616 | tf_op jit(solution)/shard_map/ppermute | solution.py:26
  44.2 42.6 %collective-permute-start = (f32[1,8,2,8,128]{4,3,2,1,0:T(8,128)S(1)}, f32[1,8,2,8,128]{4,3,2,1,0:T(8,128)S(1)}, u32[]{:S(2)}, u32[]{:S(2)}) collective-permute-start(f32[1,8,2,8,128]{4,3,2,1,0:T(8,128)S(1)} %reshape_reshape.6), channel_id=1, source_target_pairs={{16,0},{0,16},{17,1},{1,17},{18,2},{2,18},{19,3},{3,19},{20,4},{4,... | collective-permute-start | bytes 196616 | tf_op jit(solution)/shard_map/ppermute | solution.py:28
  86.9 5.5 %collective-permute-start.2 = (f32[3,8,1,8,128]{4,3,2,1,0:T(8,128)S(1)}, f32[3,8,1,8,128]{4,3,2,1,0:T(8,128)S(1)}, u32[]{:S(2)}, u32[]{:S(2)}) collective-permute-start(f32[3,8,1,8,128]{4,3,2,1,0:T(8,128)S(1)} %get-tuple-element.153), channel_id=1, source_target_pairs={{4,0},{8,4},{12,8},{0,12},{5,1},{9,5},{13,9},{1,13},{6,2},{10,6},{... | collective-permute-start | bytes 294920 | tf_op jit(solution)/shard_map/ppermute | solution.py:28
  89.2 6.3 %collective-permute-start.3 = (f32[3,8,1,8,128]{4,3,2,1,0:T(8,128)S(1)}, f32[3,8,1,8,128]{4,3,2,1,0:T(8,128)S(1)}, u32[]{:S(2)}, u32[]{:S(2)}) collective-permute-start(f32[3,8,1,8,128]{4,3,2,1,0:T(8,128)S(1)} %get-tuple-element.152), channel_id=1, source_target_pairs={{0,4},{4,8},{8,12},{12,0},{1,5},{5,9},{9,13},{13,1},{2,6},{6,10},{... | collective-permute-start | bytes 294920 | tf_op jit(solution)/shard_map/ppermute | solution.py:26
  95.6 4.1 collective-permute-start.4
  97.9 5.9 %collective-permute-start.5 = (f32[3,8,4,1,128]{4,3,2,1,0:T(1,128)S(1)}, f32[3,8,4,1,128]{4,3,2,1,0:T(1,128)S(1)}, u32[]{:S(2)}, u32[]{:S(2)}) collective-permute-start(f32[3,8,4,1,128]{4,3,2,1,0:T(1,128)S(1)} %get-tuple-element.144), channel_id=1, source_target_pairs={{0,1},{1,2},{2,3},{3,0},{4,5},{5,6},{6,7},{7,4},{8,9},{9,10},{10,1... | collective-permute-start | bytes 147464 | tf_op jit(solution)/shard_map/ppermute | solution.py:26
  107.9 20.4 %copy-start = (f32[1,1,1,9,1,32,32,128]{6,5,3,7,4,2,1,0:T(8,128)S(1)}, f32[1,1,1,9,1,32,32,128]{6,5,3,7,4,2,1,0:T(8,128)}, u32[]{:S(2)}) copy-start(f32[1,1,1,9,1,32,32,128]{6,5,3,7,4,2,1,0:T(8,128)} %copy.256) | copy-start | bytes 14155780
  128.3 36.8 %slice-start = ((s8[18874368]{0:T(1024)(128)(4,1)}), s8[2097152]{0:T(1024)(128)(4,1)S(1)}, s32[]{:S(2)}) async-start(s8[18874368]{0:T(1024)(128)(4,1)} %bitcast.514), calls=%async_computation | async-start | bytes 4194304
  128.3 36.8 %slice-start.1 = ((s8[18874368]{0:T(1024)(128)(4,1)}), s8[4194304]{0:T(1024)(128)(4,1)S(1)}, s32[]{:S(2)}) async-start(s8[18874368]{0:T(1024)(128)(4,1)} %bitcast.514), calls=%async_computation.1 | async-start | bytes 8388608
  128.3 36.7 %slice-start.2 = ((s8[18874368]{0:T(1024)(128)(4,1)}), s8[4194304]{0:T(1024)(128)(4,1)S(1)}, s32[]{:S(2)}) async-start(s8[18874368]{0:T(1024)(128)(4,1)} %bitcast.514), calls=%async_computation.2 | async-start | bytes 8388608
  145.5 19.6 %slice-start.3 = ((s8[18874368]{0:T(1024)(128)(4,1)}), s8[4194304]{0:T(1024)(128)(4,1)S(1)}, s32[]{:S(2)}) async-start(s8[18874368]{0:T(1024)(128)(4,1)} %bitcast.514), calls=%async_computation.3 | async-start | bytes 8388608
  145.5 19.6 %slice-start.4 = ((s8[18874368]{0:T(1024)(128)(4,1)}), s8[4194304]{0:T(1024)(128)(4,1)S(1)}, s32[]{:S(2)}) async-start(s8[18874368]{0:T(1024)(128)(4,1)} %bitcast.514), calls=%async_computation.4 | async-start | bytes 8388608
  261.9 1.4 collective-permute-start.7
  262.0 1.4 collective-permute-start.6
  263.4 6.3 %collective-permute-start.8 = (f32[3,8,1,8,128]{4,3,2,1,0:T(8,128)S(1)}, f32[3,8,1,8,128]{4,3,2,1,0:T(8,128)S(1)}, u32[]{:S(2)}, u32[]{:S(2)}) collective-permute-start(f32[3,8,1,8,128]{4,3,2,1,0:T(8,128)S(1)} %get-tuple-element.151), channel_id=1, source_target_pairs={{4,0},{8,4},{12,8},{0,12},{5,1},{9,5},{13,9},{1,13},{6,2},{10,6},{... | collective-permute-start | bytes 294920 | tf_op jit(solution)/shard_map/ppermute | solution.py:28
  266.6 5.8 %collective-permute-start.9 = (f32[3,8,1,8,128]{4,3,2,1,0:T(8,128)S(1)}, f32[3,8,1,8,128]{4,3,2,1,0:T(8,128)S(1)}, u32[]{:S(2)}, u32[]{:S(2)}) collective-permute-start(f32[3,8,1,8,128]{4,3,2,1,0:T(8,128)S(1)} %get-tuple-element.150), channel_id=1, source_target_pairs={{0,4},{4,8},{8,12},{12,0},{1,5},{5,9},{9,13},{13,1},{2,6},{6,10},{... | collective-permute-start | bytes 294920 | tf_op jit(solution)/shard_map/ppermute | solution.py:26
  272.4 4.1 collective-permute-start.10
  274.0 5.9 %collective-permute-start.11 = (f32[3,8,4,1,128]{4,3,2,1,0:T(1,128)S(1)}, f32[3,8,4,1,128]{4,3,2,1,0:T(1,128)S(1)}, u32[]{:S(2)}, u32[]{:S(2)}) collective-permute-start(f32[3,8,4,1,128]{4,3,2,1,0:T(1,128)S(1)} %get-tuple-element.140), channel_id=1, source_target_pairs={{0,1},{1,2},{2,3},{3,0},{4,5},{5,6},{6,7},{7,4},{8,9},{9,10},{10,1... | collective-permute-start | bytes 147464 | tf_op jit(solution)/shard_map/ppermute | solution.py:26
where the time goes:
time: 455 us; the launch traced here: 448 us
  blocking collectives  199 us (44%)
  matrix products  153 us (34%)
  local copies, waits for them, and re-layouts  59.9 us (13%)
  waiting for transfers between devices  21.8 us (5%)
  starting transfers between devices  11 us (2%)
    dot_general x8, matrix products, stacked_product(): jnp.einsum('...kcds,...ksrd->...src', blocks, field, precision=lax.Precis...  152 us
    psum x2, blocking collectives, shards(): lax.psum(column_sums(work_real * work_real + work_imag * work_imag), ('xy...  83.6 us
    psum x2, blocking collectives, shards(): proj_real, proj_imag = lax.psum((proj_real, proj_imag), ('xy', 'gz', 'ta'))  73.7 us
    psum x1, blocking collectives, shards(): lax.psum(column_sums(rhs_real * rhs_real + rhs_imag * rhs_imag), ('xy', '...  41.9 us
    unnamed x35, local copies, waits for them, and re-layouts  34.4 us
    ppermute x6, waiting for transfers between devices, padded_2(): lax.ppermute(tail, axis, [(i, (i + 1) % count) for i in range(count)])  13.1 us
    ppermute x6, starting transfers between devices, padded_2(): lax.ppermute(head, axis, [((i + 1) % count, i) for i in range(count)])  10.3 us
  transfers between devices with their start and end apart: 12, of which 9 were waited for; matrix products, arithmetic and copies ran while one was open for 10% of the time, Pallas kernels for 0%

commit v1 on v0

v1 whole, which is shorter than its diff:
```python
import functools

import jax
import jax.numpy as jnp
from jax import lax
from jax.experimental import pallas as pl
from jax.experimental.pallas import tpu as pltpu
from jax.sharding import PartitionSpec as P

DOF = 32
RHS = 2
NY = 8
CZ = 2
CT = 8
S = 128
E = 128
MESH = pl.DeviceIdType.MESH

mass_shift = 4.0
epsilon = 1e-06


def cmul(a, b):
    return (a[0] * b[0] - a[1] * b[1], a[0] * b[1] + a[1] * b[0])


def conj(a):
    return (a[0], -a[1])


def cadd(a, b):
    return (a[0] + b[0], a[1] + b[1])


def csub(a, b):
    return (a[0] - b[0], a[1] - b[1])


def scale(a, x):
    return (a[0] * x, a[1] * x)


def size2(a):
    return a[0] * a[0] + a[1] * a[1]


def coefficients(g00, g11, g22, g01, g02, g12):
    beta2 = g00 + epsilon
    beta = jnp.sqrt(beta2)
    inv_beta2 = 1.0 / beta2
    h00 = scale((mass_shift * g00 + g01[0], g01[1]), inv_beta2)
    a = (mass_shift - h00[0], -h00[1])
    left = g11 + size2(a) * g00 + 2.0 * cmul(conj(a), g01)[0]
    h10_2 = jnp.maximum(left, 0.0) * inv_beta2 + epsilon
    h10 = jnp.sqrt(h10_2)
    a4 = (a[0] + mass_shift, a[1])
    a_4 = scale(a, mass_shift)
    top = cadd(cadd(g02, cmul(a4, g01)), scale(a_4, g00))
    h01 = scale(top, inv_beta2 / h10)
    low = cadd(cadd(g12, scale(a4, g11)), cmul(a_4, conj(g01)))
    h11 = scale(cadd(low, cmul(conj(a), top)), inv_beta2 / h10_2)
    p = csub(a4, h11)
    q = csub(csub(a_4, scale(h01, h10)), cmul(h11, a))
    left = g22 + size2(p) * g11 + size2(q) * g00
    left = left + 2.0 * (
        cmul(p, conj(g12))[0] + cmul(q, conj(g02))[0] + cmul(cmul(conj(q), p), g01)[0]
    )
    h21_2 = jnp.maximum(left, 0.0) * (inv_beta2 / h10_2) + epsilon
    m00 = size2(h00) + h10_2
    m01 = cadd(cmul(conj(h00), h01), scale(h11, h10))
    m11 = size2(h01) + size2(h11) + h21_2
    t0 = scale(conj(h00), beta)
    t1 = scale(conj(h01), beta)
    inv_l0 = 1.0 / jnp.sqrt(m00)
    l10 = scale(conj(m01), inv_l0)
    f0 = scale(t0, inv_l0)
    inv_d = 1.0 / (m11 - size2(l10))
    y1 = scale(csub(t1, cmul(l10, f0)), inv_d)
    y0 = scale(csub(f0, cmul(conj(l10), y1)), inv_l0)
    inv_beta = 1.0 / beta
    wb = scale(y1, inv_beta / h10)
    wa = cadd(scale(y0, inv_beta), cmul(wb, a))
    return wa, wb


def kernel(
    sizes, b_hbm, l_hbm, sol_ref, res_ref,
    links, field, xbuf, zbuf, tface, tbuf, turned, acc, part, red1, red2,
    b_sem, l_sem, send_sem, recv_sem, s1_send, s1_recv, s2_send, s2_recv,
):
    nx, nz, nt = sizes
    group = nx * nz
    ix, iz, it = lax.axis_index("xy"), lax.axis_index("gz"), lax.axis_index("ta")
    here = ix * nz + iz

    def step(axis_value, by, count):
        return lax.rem(axis_value + (by + count), count)

    def mate(delta):
        other = lax.rem(here + delta, group)
        return (other // nz, lax.rem(other, nz), it)

    order = [0, 3, 4, 1, 2, 7, 8, 5, 6]
    b_copy = pltpu.make_async_copy(b_hbm.at[0, 0, 0], field.at[0], b_sem)
    b_copy.start()
    l_copies = {}
    for k in order:
        l_copies[k] = pltpu.make_async_copy(l_hbm.at[0, 0, 0, k], links.at[k], l_sem.at[k])
        l_copies[k].start()

    barrier = pltpu.get_barrier_semaphore()
    for delta in range(1, group):
        pl.semaphore_signal(barrier, inc=1, device_id=mate(delta), device_id_type=MESH)
    for delta in range(1, nt):
        pl.semaphore_signal(
            barrier, inc=1, device_id=(ix, iz, step(it, delta, nt)), device_id_type=MESH
        )
    pl.semaphore_wait(barrier, group - 1 + nt - 1)
    b_copy.wait()

    lane = lax.broadcasted_iota(jnp.int32, (S, E), 1)
    in_t = lane % CT
    in_z = (lane // CT) % CZ
    row8 = lax.broadcasted_iota(jnp.int32, (8, 128), 0)

    def halo(n):
        mine = field.at[n]
        tface[n, 0] = field[n, pl.ds(0, NY * CZ, stride=CT), :]
        tface[n, 1] = field[n, pl.ds(CT - 1, NY * CZ, stride=CT), :]
        tiles = mine.reshape(NY, CZ, CT, E)
        moves = []
        for way in (0, 1):
            by = 1 if way else -1
            moves.append(
                ("z%d" % way, tiles.at[:, way * (CZ - 1)], zbuf.at[n].reshape(NY, CZ, CT, E).at[:, (1 - way) * (CZ - 1)],
                 (ix, step(iz, by, nz), it))
            )
        for way in (0, 1):
            by = 1 if way else -1
            moves.append(("t%d" % way, tface.at[n, way], tbuf.at[n, way], (ix, iz, step(it, by, nt))))
        for way in (0, 1) if nx > 2 else (0,):
            by = 1 if way else -1
            moves.append(("x%d" % way, mine, xbuf.at[n, way], (step(ix, by, nx), iz, it)))
        copies = {}
        for number, (name, source, target, device) in enumerate(moves):
            copy = pltpu.make_async_remote_copy(
                src_ref=source, dst_ref=target,
                send_sem=send_sem.at[n, number], recv_sem=recv_sem.at[n, number],
                device_id=device, device_id_type=MESH,
            )
            copy.start()
            copies[name] = copy
        return copies

    def products(ks, fresh, merge, keep):
        def body(c, carry):
            if fresh:
                sums = [jnp.zeros((8, 128), jnp.float32) for _ in range(4)]
            else:
                sums = [acc[i, c] for i in range(4)]
            for k in ks:
                for j in range(DOF // 8):
                    rows = pl.ds(8 * j, 8)
                    lr = links[k, 0, c, rows, :]
                    li = links[k, 1, c, rows, :]
                    if merge:
                        lr = lr + links[k + 1, 0, c, rows, :]
                        li = li + links[k + 1, 1, c, rows, :]
                        if keep:
                            links[k, 0, c, rows, :] = lr
                            links[k, 1, c, rows, :] = li
                    for r in range(RHS):
                        vr = turned[k, pl.ds(2 * r * DOF + 8 * j, 8), :]
                        vi = turned[k, pl.ds((2 * r + 1) * DOF + 8 * j, 8), :]
                        sums[2 * r] = sums[2 * r] + lr * vr - li * vi
                        sums[2 * r + 1] = sums[2 * r + 1] + lr * vi + li * vr
            for i in range(4):
                acc[i, c] = sums[i]
            return carry

        lax.fori_loop(0, DOF, body, 0, unroll=2)

    def fold(xs):
        low = row8 < 4
        ys = [
            jnp.where(low, xs[i], xs[i + 4]) + pltpu.roll(jnp.where(low, xs[i + 4], xs[i]), 4, 0)
            for i in range(4)
        ]
        low = row8 % 4 < 2
        zs = [
            jnp.where(low, ys[i] + pltpu.roll(ys[i], 6, 0), ys[i + 2] + pltpu.roll(ys[i + 2], 2, 0))
            for i in range(2)
        ]
        return jnp.where(
            row8 % 2 < 1, zs[0] + pltpu.roll(zs[0], 7, 0), zs[1] + pltpu.roll(zs[1], 1, 0)
        )

    def apply(n, copies):
        own = turned[0]
        turned[3] = pltpu.roll(own, S - CZ * CT, 1)
        turned[4] = pltpu.roll(own, CZ * CT, 1)
        if n == 0:
            for k in (0, 3, 4):
                l_copies[k].wait()
        products((0, 3, 4), True, False, False)
        turned[5] = pltpu.roll(turned[0], S - CT, 1)
        turned[6] = pltpu.roll(turned[0], CT, 1)
        turned[7] = pltpu.roll(turned[0], S - 1, 1)
        turned[8] = pltpu.roll(turned[0], 1, 1)
        if n == 0:
            for k in (1, 2, 7, 8, 5, 6):
                l_copies[k].wait()
        copies["x0"].wait_recv()
        turned[1] = xbuf[n, 0].T
        if nx > 2:
            copies["x1"].wait_recv()
            turned[2] = xbuf[n, 1].T
            products((1, 2), False, False, False)
        else:
            products((1,), False, n == 0, n == 0)
        copies["t0"].wait_recv()
        copies["t1"].wait_recv()
        edge = field.at[3]
        edge[pl.ds(CT - 1, NY * CZ, stride=CT), :] = tbuf[n, 0]
        edge[pl.ds(0, NY * CZ, stride=CT), :] = tbuf[n, 1]
        edges = edge[...].T
        turned[7] = jnp.where(in_t == CT - 1, edges, turned[7])
        turned[8] = jnp.where(in_t == 0, edges, turned[8])
        copies["z0"].wait_recv()
        copies["z1"].wait_recv()
        edges = zbuf[n].T
        turned[5] = jnp.where(in_z == CZ - 1, edges, turned[5])
        turned[6] = jnp.where(in_z == 0, edges, turned[6])
        products((7, 8, 5, 6), False, False, False)
        for i in range(4):
            for c in range(0, DOF, 8):
                turned[0, pl.ds(i * DOF + c, 8), :] = fold([acc[i, c + j] for j in range(8)])
        field[n + 1] = turned[0].T

    field[3] = jnp.zeros((S, E), jnp.float32)
    first = halo(0)
    turned[0] = field[0].T
    apply(0, first)
    second = halo(1)
    apply(1, second)

    in_p = (lax.broadcasted_iota(jnp.int32, (S, E), 1) // DOF) % 2

    def aside(v):
        return jnp.where(in_p == 0, pltpu.roll(v, E - DOF, 1), -pltpu.roll(v, DOF, 1))

    def total(u, v):
        return jnp.sum((u * v).reshape(S // 8, 8, E), axis=0)

    k0, k1, k2 = field[0], field[1], field[2]
    z1, z2 = aside(k1), aside(k2)
    zero = jnp.zeros((8, 128), jnp.float32)
    sums = [
        total(k0, k0), total(k1, k1), total(k2, k2), total(k0, k1), total(k0, z1),
        total(k0, k2), total(k0, z2), total(k1, k2),
    ]
    part[0] = fold(sums)
    part[1] = fold([total(k1, z2)] + [zero] * 7)

    def exchange(count, target, sends, recvs, device):
        copies = []
        for delta in range(1, count):
            copies.append(
                pltpu.make_async_remote_copy(
                    src_ref=target.at[0], dst_ref=target.at[delta],
                    send_sem=sends.at[delta], recv_sem=recvs.at[delta],
                    device_id=device(delta), device_id_type=MESH,
                )
            )
        for copy in copies:
            copy.start()
        value = target[0]
        for copy in copies:
            copy.wait_recv()
        for delta in range(1, count):
            value = value + target[delta]
        return copies, value

    red1[0] = part[...]
    sent1, value = exchange(group, red1, s1_send, s1_recv, mate)
    red2[0] = value
    sent2, value = exchange(
        nt, red2, s2_send, s2_recv, lambda delta: (ix, iz, step(it, delta, nt))
    )
    value = value.reshape(16, 128)
    half = lax.broadcasted_iota(jnp.int32, (16, 128), 1) < 2 * DOF
    sum0 = jnp.sum(jnp.where(half, value, 0.0), axis=1, keepdims=True)
    sum1 = jnp.sum(jnp.where(half, 0.0, value), axis=1, keepdims=True)
    gram = jnp.where(half, sum0, sum1)
    g = [gram[i : i + 1] for i in range(9)]
    wa, wb = coefficients(g[0], g[1], g[2], (g[3], g[4]), (g[5], g[6]), (g[7], g[8]))

    def weighted(w, v, z):
        return w[0] * v - w[1] * z

    k0, k1, k2 = field[0], field[1], field[2]
    z0, z1, z2 = aside(k0), aside(k1), aside(k2)
    sol = weighted(wa, k0, z0) + weighted(wb, k1, z1)
    image = weighted(wa, k1, z1) + weighted(wb, k2, z2)
    sol_ref[0, 0, 0] = sol
    res_ref[0, 0, 0] = k0 - mass_shift * sol - image
    for copies in (first, second):
        for copy in copies.values():
            copy.wait_send()
    for copy in sent1 + sent2:
        copy.wait_send()


def shards(sizes, right_side, link_blocks):
    nx, nz, nt = sizes
    out = jax.ShapeDtypeStruct(right_side.shape, jnp.float32)
    f32 = jnp.float32
    moves = 6 if nx > 2 else 5
    return pl.pallas_call(
        functools.partial(kernel, sizes),
        out_shape=(out, out),
        in_specs=[pl.BlockSpec(memory_space=pl.ANY)] * 2,
        out_specs=(pl.BlockSpec(memory_space=pltpu.VMEM),) * 2,
        scratch_shapes=[
            pltpu.VMEM((9, 2, DOF, DOF, S), f32),
            pltpu.VMEM((4, S, E), f32),
            pltpu.VMEM((2, 2, S, E), f32),
            pltpu.VMEM((2, S, E), f32),
            pltpu.VMEM((2, 2, NY * CZ, E), f32),
            pltpu.VMEM((2, 2, NY * CZ, E), f32),
            pltpu.VMEM((9, E, S), f32),
            pltpu.VMEM((4, DOF, 8, S), f32),
            pltpu.VMEM((2, 8, 128), f32),
            pltpu.VMEM((nx * nz, 2, 8, 128), f32),
            pltpu.VMEM((nt, 2, 8, 128), f32),
            pltpu.SemaphoreType.DMA,
            pltpu.SemaphoreType.DMA((9,)),
            pltpu.SemaphoreType.DMA((2, moves)),
            pltpu.SemaphoreType.DMA((2, moves)),
            pltpu.SemaphoreType.DMA((nx * nz,)),
            pltpu.SemaphoreType.DMA((nx * nz,)),
            pltpu.SemaphoreType.DMA((nt,)),
            pltpu.SemaphoreType.DMA((nt,)),
        ],
        compiler_params=pltpu.CompilerParams(
            collective_id=0, has_side_effects=True, vmem_limit_bytes=60 * 1024 * 1024
        ),
    )(right_side, link_blocks)


def solution(mesh):
    sizes = tuple(mesh.shape[name] for name in ("xy", "gz", "ta"))
    return jax.shard_map(
        functools.partial(shards, sizes),
        mesh=mesh,
        in_specs=(
            P("xy", "gz", "ta", None, None),
            P("xy", "gz", "ta", None, None, None, None, None),
        ),
        out_specs=(P("xy", "gz", "ta", None, None), P("xy", "gz", "ta", None, None)),
        check_vma=False,
    )
```

time: 455 us -> 30.4 us (0.07); the launches traced: 448 us -> 30.2 us
  blocking collectives: 199 us -> 0 us
  matrix products: 153 us -> 0 us
  local copies, waits for them, and re-layouts: 59.9 us -> 2.95 us
  Pallas kernels: 0 us -> 26.6 us
  waiting for transfers between devices: 21.8 us -> 0 us
  starting transfers between devices: 11 us -> 0 us
    psum x5 -> x0, blocking collectives: 199 us -> none  [the longest x2 83.6 us: shards(): lax.psum(column_sums(work_real * work_real + work_imag * work_imag), ('xy...]
    dot_general x12 -> x0, matrix products: 153 us -> none  [the longest x8 152 us: stacked_product(): jnp.einsum('...kcds,...ksrd->...src', blocks, field, precision=lax.Precis...]
    unnamed x35 -> x2, local copies, waits for them, and re-layouts: 34.4 us -> 2.95 us
    pallas_call x0 -> x1, Pallas kernels: none -> 26.6 us  [shards(): pl.pallas_call(functools.partial(kernel, sizes), out_shape=(out, out), in...]
    ppermute x12 -> x0, waiting for transfers between devices: 21.8 us -> none  [the longest x6 13.1 us: padded_2(): lax.ppermute(tail, axis, [(i, (i + 1) % count) for i in range(count)])]
    another operation x46 -> x0, local copies, waits for them, and re-layouts: 12.6 us -> none
    ppermute x12 -> x0, starting transfers between devices: 11 us -> none  [the longest x6 10.3 us: padded_2(): lax.ppermute(head, axis, [((i + 1) % count, i) for i in range(count)])]
    slice x9 -> x0, local copies, waits for them, and re-layouts: 9.27 us -> none  [the longest x1 8.86 us: apply_operator(): blocks_real = link_blocks[..., 0, :, :, :]]
  transfers between devices with their start and end apart: 12 -> 0, of which waited for: 9 -> 0; matrix products, arithmetic and copies ran while one was open for 10% -> 0% of each run, Pallas kernels for 0% -> 0%
where the time goes in v1:
time: 30.4 us; the launch traced here: 30.2 us
  Pallas kernels  26.6 us (88%)
  local copies, waits for them, and re-layouts  2.95 us (10%)
  between operations  0.64 us (2%)
    pallas_call x1, Pallas kernels, shards(): pl.pallas_call(functools.partial(kernel, sizes), out_shape=(out, out), in...  26.6 us
    unnamed x2, local copies, waits for them, and re-layouts  2.95 us

profile of v1, /device:TPU:0, one launch (start us, length us, event | category | flops | bytes accessed | tf_op | source)
XLA Modules:
  0.0 30.2 jit_solution(15936179717385934444)
XLA Ops:
  0.6 26.6 %shard_map.41 = (f32[1,1,1,128,128]{4,3,2,1,0:T(8,128)}, f32[1,1,1,128,128]{4,3,2,1,0:T(8,128)}) custom-call(f32[1,1,1,128,128]{4,3,2,1,0:T(8,128)} %b_hbm.1, f32[1,1,1,9,2,32,32,128]{7,6,5,4,3,2,1,0:T(8,128)} %l_hbm.1), custom_call_target="tpu_custom_call" | custom-call | tf_op jit(solution)/shard_map/pallas_call | solution.py:319
  27.2 1.5 %copy.6 = f32[1,1,1,128,128]{4,3,2,1,0:T(8,128)} copy(f32[1,1,1,128,128]{4,3,2,1,0:T(8,128)} %get-tuple-element.4) | data formatting | bytes 131072
  28.7 1.5 %copy.7 = f32[1,1,1,128,128]{4,3,2,1,0:T(8,128)} copy(f32[1,1,1,128,128]{4,3,2,1,0:T(8,128)} %get-tuple-element.5) | data formatting | bytes 131072

commit v2 on v1

--- a/solution.py
+++ b/solution.py
@@ -131,13 +131,13 @@
         moves = []
         for way in (0, 1):
             by = 1 if way else -1
+            moves.append(("t%d" % way, tface.at[n, way], tbuf.at[n, way], (ix, iz, step(it, by, nt))))
+        for way in (0, 1):
+            by = 1 if way else -1
             moves.append(
                 ("z%d" % way, tiles.at[:, way * (CZ - 1)], zbuf.at[n].reshape(NY, CZ, CT, E).at[:, (1 - way) * (CZ - 1)],
                  (ix, step(iz, by, nz), it))
             )
-        for way in (0, 1):
-            by = 1 if way else -1
-            moves.append(("t%d" % way, tface.at[n, way], tbuf.at[n, way], (ix, iz, step(it, by, nt))))
         for way in (0, 1) if nx > 2 else (0,):
             by = 1 if way else -1
             moves.append(("x%d" % way, mine, xbuf.at[n, way], (step(ix, by, nx), iz, it)))
@@ -152,30 +152,48 @@
             copies[name] = copy
         return copies
 
-    def products(ks, fresh, merge, keep):
+    def products(passes, fresh, merge=False):
         def body(c, carry):
             if fresh:
                 sums = [jnp.zeros((8, 128), jnp.float32) for _ in range(4)]
             else:
                 sums = [acc[i, c] for i in range(4)]
-            for k in ks:
+            for link, near in passes:
                 for j in range(DOF // 8):
                     rows = pl.ds(8 * j, 8)
-                    lr = links[k, 0, c, rows, :]
-                    li = links[k, 1, c, rows, :]
+                    lr = links[link, 0, c, rows, :]
+                    li = links[link, 1, c, rows, :]
                     if merge:
-                        lr = lr + links[k + 1, 0, c, rows, :]
-                        li = li + links[k + 1, 1, c, rows, :]
-                        if keep:
-                            links[k, 0, c, rows, :] = lr
-                            links[k, 1, c, rows, :] = li
+                        lr = lr + links[link + 1, 0, c, rows, :]
+                        li = li + links[link + 1, 1, c, rows, :]
+                        links[link, 0, c, rows, :] = lr
+                        links[link, 1, c, rows, :] = li
                     for r in range(RHS):
-                        vr = turned[k, pl.ds(2 * r * DOF + 8 * j, 8), :]
-                        vi = turned[k, pl.ds((2 * r + 1) * DOF + 8 * j, 8), :]
+                        vr = turned[near, pl.ds(2 * r * DOF + 8 * j, 8), :]
+                        vi = turned[near, pl.ds((2 * r + 1) * DOF + 8 * j, 8), :]
                         sums[2 * r] = sums[2 * r] + lr * vr - li * vi
                         sums[2 * r + 1] = sums[2 * r + 1] + lr * vi + li * vr
             for i in range(4):
                 acc[i, c] = sums[i]
+            return carry
+
+        lax.fori_loop(0, DOF, body, 0, unroll=2)
+
+    lane8 = lax.broadcasted_iota(jnp.int32, (8, 128), 1)
+
+    def split_links():
+        inner = (lane8 // CT) % CZ == 0
+        last = lane8 % CT == CT - 1
+
+        def body(c, carry):
+            for p in range(2):
+                for j in range(DOF // 8):
+                    rows = pl.ds(8 * j, 8)
+                    up, down = links[5, p, c, rows, :], links[6, p, c, rows, :]
+                    links[5, p, c, rows, :] = jnp.where(inner, up, down)
+                    links[6, p, c, rows, :] = jnp.where(inner, down, up)
+                    up, down = links[7, p, c, rows, :], links[8, p, c, rows, :]
+                    links[9, p, c, rows, :] = jnp.where(last, up, down)
             return carry
 
         lax.fori_loop(0, DOF, body, 0, unroll=2)
@@ -199,39 +217,34 @@
         own = turned[0]
         turned[3] = pltpu.roll(own, S - CZ * CT, 1)
         turned[4] = pltpu.roll(own, CZ * CT, 1)
+        turned[5] = jnp.where(in_z == 0, pltpu.roll(own, S - CT, 1), pltpu.roll(own, CT, 1))
+        turned[7] = jnp.where(in_t == CT - 1, 0.0, pltpu.roll(own, S - 1, 1))
+        turned[8] = jnp.where(in_t == 0, 0.0, pltpu.roll(own, 1, 1))
         if n == 0:
-            for k in (0, 3, 4):
+            for k in range(9):
                 l_copies[k].wait()
-        products((0, 3, 4), True, False, False)
-        turned[5] = pltpu.roll(turned[0], S - CT, 1)
-        turned[6] = pltpu.roll(turned[0], CT, 1)
-        turned[7] = pltpu.roll(turned[0], S - 1, 1)
-        turned[8] = pltpu.roll(turned[0], 1, 1)
-        if n == 0:
-            for k in (1, 2, 7, 8, 5, 6):
-                l_copies[k].wait()
+            split_links()
+        products(((0, 0), (3, 3), (4, 4)), True)
+        products(((5, 5), (7, 7), (8, 8)), False)
         copies["x0"].wait_recv()
         turned[1] = xbuf[n, 0].T
         if nx > 2:
             copies["x1"].wait_recv()
             turned[2] = xbuf[n, 1].T
-            products((1, 2), False, False, False)
+            products(((1, 1), (2, 2)), False)
         else:
-            products((1,), False, n == 0, n == 0)
+            products(((1, 1),), False, n == 0)
+        copies["z0"].wait_recv()
+        copies["z1"].wait_recv()
+        turned[6] = zbuf[n].T
+        products(((6, 6),), False)
         copies["t0"].wait_recv()
         copies["t1"].wait_recv()
         edge = field.at[3]
         edge[pl.ds(CT - 1, NY * CZ, stride=CT), :] = tbuf[n, 0]
         edge[pl.ds(0, NY * CZ, stride=CT), :] = tbuf[n, 1]
-        edges = edge[...].T
-        turned[7] = jnp.where(in_t == CT - 1, edges, turned[7])
-        turned[8] = jnp.where(in_t == 0, edges, turned[8])
-        copies["z0"].wait_recv()
-        copies["z1"].wait_recv()
-        edges = zbuf[n].T
-        turned[5] = jnp.where(in_z == CZ - 1, edges, turned[5])
-        turned[6] = jnp.where(in_z == 0, edges, turned[6])
-        products((7, 8, 5, 6), False, False, False)
+        turned[9] = edge[...].T
+        products(((9, 9),), False)
         for i in range(4):
             for c in range(0, DOF, 8):
                 turned[0, pl.ds(i * DOF + c, 8), :] = fold([acc[i, c + j] for j in range(8)])
@@ -254,13 +267,17 @@
 
     k0, k1, k2 = field[0], field[1], field[2]
     z1, z2 = aside(k1), aside(k2)
-    zero = jnp.zeros((8, 128), jnp.float32)
     sums = [
         total(k0, k0), total(k1, k1), total(k2, k2), total(k0, k1), total(k0, z1),
-        total(k0, k2), total(k0, z2), total(k1, k2),
+        total(k0, k2), total(k0, z2),
     ]
-    part[0] = fold(sums)
-    part[1] = fold([total(k1, z2)] + [zero] * 7)
+    first_p = in_p[:8] == 0
+
+    def both(v):
+        return v + jnp.where(first_p, pltpu.roll(v, E - DOF, 1), pltpu.roll(v, DOF, 1))
+
+    sums.append(jnp.where(first_p, both(total(k1, k2)), both(total(k1, z2))))
+    part[...] = fold(sums)
 
     def exchange(count, target, sends, recvs, device):
         copies = []
@@ -287,12 +304,15 @@
     sent2, value = exchange(
         nt, red2, s2_send, s2_recv, lambda delta: (ix, iz, step(it, delta, nt))
     )
-    value = value.reshape(16, 128)
-    half = lax.broadcasted_iota(jnp.int32, (16, 128), 1) < 2 * DOF
-    sum0 = jnp.sum(jnp.where(half, value, 0.0), axis=1, keepdims=True)
-    sum1 = jnp.sum(jnp.where(half, 0.0, value), axis=1, keepdims=True)
-    gram = jnp.where(half, sum0, sum1)
-    g = [gram[i : i + 1] for i in range(9)]
+    quarter = lax.broadcasted_iota(jnp.int32, (8, 128), 1) // DOF
+    sum00, sum01, sum10, sum11 = [
+        jnp.sum(jnp.where(quarter == i, value, 0.0), axis=1, keepdims=True) for i in range(4)
+    ]
+    half = quarter < 2
+    gram = jnp.where(half, sum00 + sum01, sum10 + sum11)
+    g = [gram[i : i + 1] for i in range(7)]
+    g.append(jnp.where(half, sum00, sum10)[7:8])
+    g.append(jnp.where(half, sum01, sum11)[7:8])
     wa, wb = coefficients(g[0], g[1], g[2], (g[3], g[4]), (g[5], g[6]), (g[7], g[8]))
 
     def weighted(w, v, z):
@@ -311,28 +331,34 @@
         copy.wait_send()
 
 
+def deliver(a_ref, b_ref, sol_ref, res_ref):
+    sol_ref[...] = a_ref[...]
+    res_ref[...] = b_ref[...]
+
+
 def shards(sizes, right_side, link_blocks):
     nx, nz, nt = sizes
     out = jax.ShapeDtypeStruct(right_side.shape, jnp.float32)
     f32 = jnp.float32
     moves = 6 if nx > 2 else 5
-    return pl.pallas_call(
+    held = pltpu.VMEM(right_side.shape, f32)
+    results = pl.pallas_call(
         functools.partial(kernel, sizes),
-        out_shape=(out, out),
+        out_shape=(held, held),
         in_specs=[pl.BlockSpec(memory_space=pl.ANY)] * 2,
         out_specs=(pl.BlockSpec(memory_space=pltpu.VMEM),) * 2,
         scratch_shapes=[
-            pltpu.VMEM((9, 2, DOF, DOF, S), f32),
+            pltpu.VMEM((10, 2, DOF, DOF, S), f32),
             pltpu.VMEM((4, S, E), f32),
             pltpu.VMEM((2, 2, S, E), f32),
             pltpu.VMEM((2, S, E), f32),
             pltpu.VMEM((2, 2, NY * CZ, E), f32),
             pltpu.VMEM((2, 2, NY * CZ, E), f32),
-            pltpu.VMEM((9, E, S), f32),
+            pltpu.VMEM((10, E, S), f32),
             pltpu.VMEM((4, DOF, 8, S), f32),
-            pltpu.VMEM((2, 8, 128), f32),
-            pltpu.VMEM((nx * nz, 2, 8, 128), f32),
-            pltpu.VMEM((nt, 2, 8, 128), f32),
+            pltpu.VMEM((8, 128), f32),
+            pltpu.VMEM((nx * nz, 8, 128), f32),
+            pltpu.VMEM((nt, 8, 128), f32),
             pltpu.SemaphoreType.DMA,
             pltpu.SemaphoreType.DMA((9,)),
             pltpu.SemaphoreType.DMA((2, moves)),
@@ -343,9 +369,15 @@
             pltpu.SemaphoreType.DMA((nt,)),
         ],
         compiler_params=pltpu.CompilerParams(
-            collective_id=0, has_side_effects=True, vmem_limit_bytes=60 * 1024 * 1024
+            collective_id=0, has_side_effects=True, vmem_limit_bytes=56 * 1024 * 1024
         ),
     )(right_side, link_blocks)
+    return pl.pallas_call(
+        deliver,
+        out_shape=(out, out),
+        in_specs=[pl.BlockSpec(memory_space=pltpu.VMEM)] * 2,
+        out_specs=(pl.BlockSpec(memory_space=pltpu.VMEM),) * 2,
+    )(*[pltpu.with_memory_space_constraint(x, pltpu.VMEM) for x in results])
 
 
 def solution(mesh):

time: 30.4 us -> 25.8 us (0.85)
  local copies, waits for them, and re-layouts: 2.95 us -> 0 us
  Pallas kernels: 26.6 us -> 25 us
    unnamed x2 -> x0, local copies, waits for them, and re-layouts: 2.95 us -> none
    pallas_call x1 -> x2, Pallas kernels: 26.6 us -> 25 us  [the longest x1 24.3 us: shards(): pl.pallas_call(functools.partial(kernel, sizes), out_shape=(held, held),...]
where the time goes in v2:
time: 25.8 us; the launch traced here: 25.6 us
  Pallas kernels  25 us (97%)
  between operations  0.64 us (2%)
    pallas_call x1, Pallas kernels, shards(): pl.pallas_call(functools.partial(kernel, sizes), out_shape=(held, held),...  24.3 us
    pallas_call x1, Pallas kernels, shards(): pl.pallas_call(deliver, out_shape=(out, out), in_specs=[pl.BlockSpec(memo...  0.66 us

profile of v2, /device:TPU:0, one launch (start us, length us, event | category | flops | bytes accessed | tf_op | source)
XLA Modules:
  0.0 25.6 jit_solution(3220938114261365103)
XLA Ops:
  0.6 24.3 %shard_map.41 = (f32[1,1,1,128,128]{4,3,2,1,0:T(8,128)S(1)}, f32[1,1,1,128,128]{4,3,2,1,0:T(8,128)S(1)}) custom-call(f32[1,1,1,128,128]{4,3,2,1,0:T(8,128)} %b_hbm.1, f32[1,1,1,9,2,32,32,128]{7,6,5,4,3,2,1,0:T(8,128)} %l_hbm.1), custom_call_target="tpu_custom_call" | custom-call | tf_op jit(solution)/shard_map/pallas_call | solution.py:345
  25.0 0.7 %shard_map.42 = (f32[1,1,1,128,128]{4,3,2,1,0:T(8,128)}, f32[1,1,1,128,128]{4,3,2,1,0:T(8,128)}) custom-call(f32[1,1,1,128,128]{4,3,2,1,0:T(8,128)S(1)} %get-tuple-element.4.a_ref, f32[1,1,1,128,128]{4,3,2,1,0:T(8,128)S(1)} %get-tuple-element.5.b_ref), custom_call_target="tpu_custom_call" | custom-call | tf_op jit(solution)/shard_map/pallas_call | solution.py:375

commit v3 on v2

--- a/solution.py
+++ b/solution.py
@@ -85,20 +85,21 @@
 
 def kernel(
     sizes, b_hbm, l_hbm, sol_ref, res_ref,
-    links, field, xbuf, zbuf, tface, tbuf, turned, acc, part, red1, red2,
-    b_sem, l_sem, send_sem, recv_sem, s1_send, s1_recv, s2_send, s2_recv,
+    links, field, xbuf, zbuf, tface, tbuf, turned, acc, red,
+    b_sem, l_sem, send_sem, recv_sem, sum_send, sum_recv,
 ):
     nx, nz, nt = sizes
-    group = nx * nz
+    total_count = nx * nz * nt
     ix, iz, it = lax.axis_index("xy"), lax.axis_index("gz"), lax.axis_index("ta")
-    here = ix * nz + iz
+    here = (ix * nz + iz) * nt + it
 
     def step(axis_value, by, count):
         return lax.rem(axis_value + (by + count), count)
 
     def mate(delta):
-        other = lax.rem(here + delta, group)
-        return (other // nz, lax.rem(other, nz), it)
+        other = lax.rem(here + delta, total_count)
+        plane = other // nt
+        return (plane // nz, lax.rem(plane, nz), lax.rem(other, nt))
 
     order = [0, 3, 4, 1, 2, 7, 8, 5, 6]
     b_copy = pltpu.make_async_copy(b_hbm.at[0, 0, 0], field.at[0], b_sem)
@@ -109,13 +110,9 @@
         l_copies[k].start()
 
     barrier = pltpu.get_barrier_semaphore()
-    for delta in range(1, group):
+    for delta in range(1, total_count):
         pl.semaphore_signal(barrier, inc=1, device_id=mate(delta), device_id_type=MESH)
-    for delta in range(1, nt):
-        pl.semaphore_signal(
-            barrier, inc=1, device_id=(ix, iz, step(it, delta, nt)), device_id_type=MESH
-        )
-    pl.semaphore_wait(barrier, group - 1 + nt - 1)
+    pl.semaphore_wait(barrier, total_count - 1)
     b_copy.wait()
 
     lane = lax.broadcasted_iota(jnp.int32, (S, E), 1)
@@ -277,33 +274,26 @@
         return v + jnp.where(first_p, pltpu.roll(v, E - DOF, 1), pltpu.roll(v, DOF, 1))
 
     sums.append(jnp.where(first_p, both(total(k1, k2)), both(total(k1, z2))))
-    part[...] = fold(sums)
-
-    def exchange(count, target, sends, recvs, device):
-        copies = []
-        for delta in range(1, count):
-            copies.append(
-                pltpu.make_async_remote_copy(
-                    src_ref=target.at[0], dst_ref=target.at[delta],
-                    send_sem=sends.at[delta], recv_sem=recvs.at[delta],
-                    device_id=device(delta), device_id_type=MESH,
-                )
-            )
-        for copy in copies:
-            copy.start()
-        value = target[0]
-        for copy in copies:
-            copy.wait_recv()
-        for delta in range(1, count):
-            value = value + target[delta]
-        return copies, value
-
-    red1[0] = part[...]
-    sent1, value = exchange(group, red1, s1_send, s1_recv, mate)
-    red2[0] = value
-    sent2, value = exchange(
-        nt, red2, s2_send, s2_recv, lambda delta: (ix, iz, step(it, delta, nt))
-    )
+    lanes = fold(sums)
+    for width in (16, 8, 4):
+        low = lane8 % (2 * width) < width
+        lanes = lanes + jnp.where(
+            low, pltpu.roll(lanes, 128 - width, 1), pltpu.roll(lanes, width, 1)
+        )
+    seat = (lane8 % DOF) // 4 == row8
+    red[0] = jnp.sum(jnp.where(seat, lanes, 0.0), axis=0, keepdims=True)
+    sent = []
+    for delta in range(1, total_count):
+        copy = pltpu.make_async_remote_copy(
+            src_ref=red.at[0], dst_ref=red.at[delta],
+            send_sem=sum_send.at[delta], recv_sem=sum_recv.at[delta],
+            device_id=mate(delta), device_id_type=MESH,
+        )
+        copy.start()
+        sent.append(copy)
+    for copy in sent:
+        copy.wait_recv()
+    value = jnp.where(seat, jnp.sum(red[...], axis=0), 0.0)
     quarter = lax.broadcasted_iota(jnp.int32, (8, 128), 1) // DOF
     sum00, sum01, sum10, sum11 = [
         jnp.sum(jnp.where(quarter == i, value, 0.0), axis=1, keepdims=True) for i in range(4)
@@ -327,7 +317,7 @@
     for copies in (first, second):
         for copy in copies.values():
             copy.wait_send()
-    for copy in sent1 + sent2:
+    for copy in sent:
         copy.wait_send()
 
 
@@ -356,17 +346,13 @@
             pltpu.VMEM((2, 2, NY * CZ, E), f32),
             pltpu.VMEM((10, E, S), f32),
             pltpu.VMEM((4, DOF, 8, S), f32),
-            pltpu.VMEM((8, 128), f32),
-            pltpu.VMEM((nx * nz, 8, 128), f32),
-            pltpu.VMEM((nt, 8, 128), f32),
+            pltpu.VMEM((nx * nz * nt, 1, 128), f32),
             pltpu.SemaphoreType.DMA,
             pltpu.SemaphoreType.DMA((9,)),
             pltpu.SemaphoreType.DMA((2, moves)),
             pltpu.SemaphoreType.DMA((2, moves)),
-            pltpu.SemaphoreType.DMA((nx * nz,)),
-            pltpu.SemaphoreType.DMA((nx * nz,)),
-            pltpu.SemaphoreType.DMA((nt,)),
-            pltpu.SemaphoreType.DMA((nt,)),
+            pltpu.SemaphoreType.DMA((nx * nz * nt,)),
+            pltpu.SemaphoreType.DMA((nx * nz * nt,)),
         ],
         compiler_params=pltpu.CompilerParams(
             collective_id=0, has_side_effects=True, vmem_limit_bytes=56 * 1024 * 1024

time: 25.8 us -> 24.2 us (0.938)
  Pallas kernels: 25 us -> 23.4 us
    pallas_call x1, Pallas kernels: 24.3 us -> 22.8 us  [shards(): pl.pallas_call(functools.partial(kernel, sizes), out_shape=(held, held),...]
where the time goes in v3:
time: 24.2 us; the launch traced here: 24.1 us
  Pallas kernels  23.4 us (97%)
  between operations  0.64 us (3%)
    pallas_call x1, Pallas kernels, shards(): pl.pallas_call(functools.partial(kernel, sizes), out_shape=(held, held),...  22.8 us
    pallas_call x1, Pallas kernels, shards(): pl.pallas_call(deliver, out_shape=(out, out), in_specs=[pl.BlockSpec(memo...  0.66 us

profile of v3, /device:TPU:0, one launch (start us, length us, event | category | flops | bytes accessed | tf_op | source)
XLA Modules:
  0.0 24.1 jit_solution(17189979057661250419)
XLA Ops:
  0.6 22.8 %shard_map.41 = (f32[1,1,1,128,128]{4,3,2,1,0:T(8,128)S(1)}, f32[1,1,1,128,128]{4,3,2,1,0:T(8,128)S(1)}) custom-call(f32[1,1,1,128,128]{4,3,2,1,0:T(8,128)} %b_hbm.1, f32[1,1,1,9,2,32,32,128]{7,6,5,4,3,2,1,0:T(8,128)} %l_hbm.1), custom_call_target="tpu_custom_call" | custom-call | tf_op jit(solution)/shard_map/pallas_call | solution.py:335
  23.4 0.7 %shard_map.42 = (f32[1,1,1,128,128]{4,3,2,1,0:T(8,128)}, f32[1,1,1,128,128]{4,3,2,1,0:T(8,128)}) custom-call(f32[1,1,1,128,128]{4,3,2,1,0:T(8,128)S(1)} %get-tuple-element.4.a_ref, f32[1,1,1,128,128]{4,3,2,1,0:T(8,128)S(1)} %get-tuple-element.5.b_ref), custom_call_target="tpu_custom_call" | custom-call | tf_op jit(solution)/shard_map/pallas_call | solution.py:361
